TPU v7x, 512 devices: a 4x2x32 block of a 4x8x32 slice. The times are simulated.
512 devices in a mesh: grp: 2 (over y), gx: 32 (over z), gy: 4 (over x), gz: 2 (over core).
Axes of the slice: x: 4, y: 2, z: 32, core: 2. Of those that a mesh axis runs over, the one named last changes fastest.
The devices are a block of a 4x8x32 slice.
Arguments:
- position: float32 [64, 128, 8, 256], P(None, ('grp', 'gx'), 'gy', 'gz'), parts along dimension 1, may hold values from -6 to 6
- momentum: float32 [64, 128, 8, 256], P(None, ('grp', 'gx'), 'gy', 'gz'), parts along dimension 1, may hold values from -6 to 6
- noise: bfloat16 [3, 64, 128, 8, 256], P(None, None, ('grp', 'gx'), 'gy', 'gz'), parts along dimension 2, may hold values from -6 to 6
- filter_in: bfloat16 [64, 64, 3, 3, 3], P('gx', 'gy'), may hold values from -0.15625 to 0.15625
- filter_out: bfloat16 [64, 64, 3, 3, 3], P('gx', 'gy'), may hold values from -0.15625 to 0.15625
- bias: float32 [64], replicated, may hold values from -4 to 4
Outputs:
- final_position: float32 [64, 128, 8, 256], P(None, ('grp', 'gx'), 'gy', 'gz'), parts along dimension 1
- final_momentum: float32 [64, 128, 8, 256], P(None, ('grp', 'gx'), 'gy', 'gz'), parts along dimension 1
There are 2 independent parts, one for each index of `grp`. A program takes and returns all parts, laid end to end along the dimension named above; an argument that names none is the same for every part. Nothing has to cross between parts.
All inputs are finite; a program needn't handle non-finite values.
Results may differ from a plain program's by a relative error of at most 0.0013.
Values may be sent and summed in bfloat16 or wider, within the bound.
A program may use at most 64 MiB of HBM per device.

v0:
```python
import jax
import jax.numpy as jnp
from jax import lax
from jax.experimental import pallas as pl
from jax.experimental.pallas import tpu as pltpu
from jax.sharding import PartitionSpec as P

MESH = pl.DeviceIdType.MESH
EDGE = 16
AROUND = [(dx, dy) for dx in (-1, 1) for dy in (-1, 1)] + [(-1, 0), (1, 0), (0, -1), (0, 1)]


def shifted_sum(parts, slot, rows, count):
    low = pltpu.roll(parts[0, slot], 1, 0)
    high = pltpu.roll(parts[2, slot], rows - 1, 0)
    return low + parts[1, slot] + high


def kernel(
    position, momentum, noise, filters, adjoints, bias, out_position, out_momentum,
    wide_in, wide_out, slim_in, slim_out, band, outer, own, own_edge, back, back_edge,
    q, p, force, active, hidden, wide_parts, slim_parts, send_sem, recv_sem,
):
    steps = noise.shape[0]
    depth, lanes = own.shape[1:]
    half = lanes // 2
    rows = band.shape[2]
    gx, gy, gz = (lax.axis_index(name) for name in ("gx", "gy", "gz"))
    nx, ny, nz = (lax.axis_size(name) for name in ("gx", "gy", "gz"))
    partner = lax.rem(gz + 1, nz)

    def at(dx, dy, z):
        return {"gx": lax.rem(gx + dx + nx, nx), "gy": lax.rem(gy + dy + ny, ny), "gz": z}

    barrier = pltpu.get_barrier_semaphore()
    for dx, dy in AROUND:
        pl.semaphore_signal(barrier, inc=1, device_id=at(dx, dy, gz), device_id_type=MESH)
        pl.semaphore_signal(barrier, inc=1, device_id=at(dx, dy, partner), device_id_type=MESH)
    pl.semaphore_signal(barrier, inc=1, device_id=at(0, 0, partner), device_id_type=MESH)
    pl.semaphore_wait(barrier, 2 * len(AROUND) + 1)

    def copies(which, block, edge, padded):
        found = []
        for n, (dx, dy) in enumerate(AROUND):
            spot = padded.at[1 - dy, pl.ds(2 - 2 * dx, 2)]
            found.append(
                pltpu.make_async_remote_copy(
                    src_ref=block, dst_ref=spot.at[:, pl.ds(0, depth)],
                    send_sem=send_sem.at[which, 2 * n], recv_sem=recv_sem.at[which, 2 * n],
                    device_id=at(dx, dy, gz), device_id_type=MESH,
                )
            )
            found.append(
                pltpu.make_async_remote_copy(
                    src_ref=edge, dst_ref=spot.at[:, pl.ds(depth, EDGE)],
                    send_sem=send_sem.at[which, 2 * n + 1], recv_sem=recv_sem.at[which, 2 * n + 1],
                    device_id=at(dx, dy, partner), device_id_type=MESH,
                )
            )
        last = 2 * len(AROUND)
        found.append(
            pltpu.make_async_remote_copy(
                src_ref=edge, dst_ref=padded.at[1, pl.ds(2, 2), pl.ds(depth, EDGE)],
                send_sem=send_sem.at[which, last], recv_sem=recv_sem.at[which, last],
                device_id=at(0, 0, partner), device_id_type=MESH,
            )
        )
        return found

    def exchange(which, value, block, edge, padded):
        row = lax.broadcasted_iota(jnp.int32, (2, EDGE, lanes), 1)
        first = value[:, :EDGE].astype(jnp.float32)
        final = value[:, depth - EDGE :].astype(jnp.float32)
        block[...] = value
        edge[...] = jnp.where(row < EDGE // 2, first, final).astype(jnp.bfloat16)
        sent = copies(which, block, edge, padded)
        for copy in sent:
            copy.start()
        padded[1, 2:4, 0:depth] = value
        for copy in sent:
            copy.wait()

    def wide(padded, weights):
        @pl.loop(0, 3)
        def _(c):
            pieces = [
                padded[y, a : a + 4].reshape(4 * rows, lanes) for a in range(3) for y in range(3)
            ]
            made = jnp.dot(
                jnp.concatenate(pieces, axis=1), weights[c], preferred_element_type=jnp.float32
            )
            wide_parts[c] = made.reshape(4, rows, 2 * lanes)

    def slim(weights):
        pieces = [hidden[a : a + 2].reshape(2 * rows, 2 * lanes) for a in range(3)]
        taps = jnp.concatenate(pieces, axis=1)
        for c in range(3):
            made = jnp.dot(taps, weights[c], preferred_element_type=jnp.float32)
            slim_parts[c] = made.reshape(2, rows, lanes)

    def banded(source, which, target, wide_one):
        target[...] = jnp.zeros_like(target)
        span = 6 if wide_one else 4

        @pl.loop(0, 9)
        def _(tap):
            c, a = tap // 3, lax.rem(tap, 3)
            taps = [source[which, a, b, c] for b in range(3)]
            zero = jnp.zeros((half, half), jnp.bfloat16)
            pairs = [
                jnp.concatenate([taps[b] if b < 3 else zero, taps[b - 1] if b > 0 else zero], axis=1)
                for b in range(4)
            ]
            for group in range(2 if wide_one else 1):
                for b in range(4):
                    start = pl.multiple_of(a * (span * half) + (2 * group + b) * half, half)
                    target[c, pl.ds(start, half), group * lanes : (group + 1) * lanes] = pairs[b]

    banded(filters, 0, wide_in, True)
    banded(filters, 1, slim_out, False)
    banded(adjoints, 1, wide_out, True)
    banded(adjoints, 0, slim_in, False)

    for x in range(2):
        q[x] = position[x].T
        p[x] = momentum[x].T

    size = 0.25
    decay = jnp.exp(jnp.float32(-0.25))
    kick = jnp.sqrt(1.0 - decay * decay)

    @pl.loop(0, steps + 1)
    def _(k):
        exchange(0, q[...].astype(jnp.bfloat16), own, own_edge, band)
        wide(band, wide_in)
        for x in range(4):
            t = jnp.tanh(shifted_sum(wide_parts, x, rows, 4) + bias[...])
            active[x] = t
            hidden[x] = t.astype(jnp.bfloat16)
        slim(slim_out)
        out = [shifted_sum(slim_parts, x, rows, 2)[:depth].astype(jnp.bfloat16) for x in range(2)]
        exchange(1, jnp.stack(out), back, back_edge, outer)
        wide(outer, wide_out)
        for x in range(4):
            t = active[x]
            gu = shifted_sum(wide_parts, x, rows, 4)
            hidden[x] = (gu * (1.0 - t * t)).astype(jnp.bfloat16)
        slim(slim_in)
        for x in range(2):
            force[x] = shifted_sum(slim_parts, x, rows, 2)[:depth] + q[x]

        @pl.when(k > 0)
        def _():
            p[...] = p[...] - 0.5 * size * force[...]

        @pl.when(k < steps)
        def _():
            for x in range(2):
                drawn = noise[lax.min(k, steps - 1), x].astype(jnp.float32).T
                moment = p[x] - 0.5 * size * force[x]
                field = q[x] + 0.5 * size * moment
                moment = decay * moment + kick * drawn
                q[x] = field + 0.5 * size * moment
                p[x] = moment

    for x in range(2):
        out_position[x] = q[x].T
        out_momentum[x] = p[x].T


def on_device(position, momentum, noise, filter_in, filter_out, bias):
    channels, nx, ny, depth = position.shape
    steps = noise.shape[0]
    lanes = ny * channels
    rows = depth + EDGE

    own = jnp.stack([filter_in, filter_out])
    two, o_own, i_own = own.shape[:3]
    flat = own.reshape(two, o_own, i_own, 27)
    every = lax.all_gather(flat, ("gx", "gy"), axis=0)
    parts_x, parts_y = lax.axis_size("gx"), lax.axis_size("gy")
    every = every.reshape(parts_x, parts_y, two, o_own, i_own, 27)
    natural = jnp.transpose(every, (2, 5, 0, 3, 1, 4)).reshape(two, 3, 3, 3, channels, channels)
    adjoints = jnp.flip(natural, (1, 2, 3))
    filters = jnp.swapaxes(natural, -1, -2)

    def to_planes(block):
        return jnp.transpose(block, (1, 2, 0, 3)).reshape(nx, lanes, depth)

    def from_planes(planes):
        return jnp.transpose(planes.reshape(nx, ny, channels, depth), (2, 0, 1, 3))

    noise_planes = jnp.transpose(noise, (0, 2, 3, 1, 4)).reshape(steps, nx, lanes, depth)
    bias_row = jnp.tile(bias, 2 * ny).reshape(1, 2 * lanes)

    bf, f32 = jnp.bfloat16, jnp.float32
    messages = 2 * len(AROUND) + 1
    planes = jax.ShapeDtypeStruct((nx, lanes, depth), f32)
    vmem = pl.BlockSpec(memory_space=pltpu.VMEM)
    final_position, final_momentum = pl.pallas_call(
        kernel,
        out_shape=(planes, planes),
        in_specs=[vmem] * 6,
        out_specs=(vmem, vmem),
        scratch_shapes=[
            pltpu.VMEM((3, 9 * lanes, 2 * lanes), bf),
            pltpu.VMEM((3, 9 * lanes, 2 * lanes), bf),
            pltpu.VMEM((3, 6 * lanes, lanes), bf),
            pltpu.VMEM((3, 6 * lanes, lanes), bf),
            pltpu.VMEM((3, 6, rows, lanes), bf),
            pltpu.VMEM((3, 6, rows, lanes), bf),
            pltpu.VMEM((nx, depth, lanes), bf),
            pltpu.VMEM((nx, EDGE, lanes), bf),
            pltpu.VMEM((nx, depth, lanes), bf),
            pltpu.VMEM((nx, EDGE, lanes), bf),
            pltpu.VMEM((nx, depth, lanes), f32),
            pltpu.VMEM((nx, depth, lanes), f32),
            pltpu.VMEM((nx, depth, lanes), f32),
            pltpu.VMEM((4, rows, 2 * lanes), f32),
            pltpu.VMEM((4, rows, 2 * lanes), bf),
            pltpu.VMEM((3, 4, rows, 2 * lanes), f32),
            pltpu.VMEM((3, 2, rows, lanes), f32),
            pltpu.SemaphoreType.DMA((2, messages)),
            pltpu.SemaphoreType.DMA((2, messages)),
        ],
        compiler_params=pltpu.CompilerParams(
            collective_id=0, has_side_effects=True, vmem_limit_bytes=40 * 1024 * 1024
        ),
        name="langevin",
    )(to_planes(position), to_planes(momentum), noise_planes, filters, adjoints, bias_row)
    return from_planes(final_position), from_planes(final_momentum)


def solution(mesh):
    field = P(None, ("grp", "gx"), "gy", "gz")
    in_specs = (
        field,
        field,
        P(None, None, ("grp", "gx"), "gy", "gz"),
        P("gx", "gy", None, None, None),
        P("gx", "gy", None, None, None),
        P(),
    )
    return jax.shard_map(
        on_device, mesh=mesh, in_specs=in_specs, out_specs=(field, field), check_vma=False
    )
```

profile of v0, /device:TPU:33, one launch (start us, length us, event | category | flops | bytes accessed | tf_op | source)
XLA Modules:
  0.0 364.9 jit_solution(17051771240861696154)
XLA Ops:
  0.6 0.8 pad_maximum_fusion
  1.4 0.1 copy.35
  1.5 212.7 %all_gather.3 = bf16[128,2,2,16,27]{4,3,2,1,0:T(8,128)(2,1)} all-gather(bf16[1,2,2,16,27]{4,3,2,1,0:T(8,128)(2,1)S(1)} %copy.35), channel_id=1, replica_groups=mesh['grp'=2,'gx'=32,'gy'=4,'gz'=2] {'gx','gy'}, dimensions={0}, use_global_device_ids=true | all-gather | bytes 445824 | tf_op jit(solution)/shard_map/all_gather | solution.py:180
  214.2 6.9 %copy.36 = bf16[2,27,32,2,4,16]{5,4,3,2,1,0:T(4,128)(2,1)S(1)} copy(bf16[2,27,32,2,4,16]{1,5,3,0,4,2:T(8,128)(2,1)} %bitcast.24) | data formatting | bytes 884736 | tf_op jit(solution)/shard_map/transpose | solution.py:183
  221.2 0.0 copy-start.3
  221.2 2.7 reshape.34
  223.9 0.0 copy-start
  223.9 0.0 copy-start.1
  223.9 0.0 copy-start.2
  223.9 1.6 copy.37
  225.5 1.2 rev.4.adjoints
  226.7 0.0 copy-done
  226.8 0.0 copy-done.1
  226.8 0.0 copy-done.2
  226.8 0.0 copy-done.3
  226.8 0.1 reshape_tile.3.bias
  226.9 137.1 %langevin.1 = (f32[2,128,128]{2,1,0:T(8,128)S(1)}, f32[2,128,128]{2,1,0:T(8,128)S(1)}) custom-call(f32[2,128,128]{2,1,0:T(8,128)S(1)} %bitcast.20, f32[2,128,128]{2,1,0:T(8,128)S(1)} %bitcast.21, bf16[3,2,128,128]{3,2,1,0:T(8,128)(2,1)S(1)} %bitcast.19, bf16[2,3,3,3,64,64]{5,4,3,2,1,0:T(8,128)(2,1)S(1)} %bitcast.18, ...), custom_call_target="tpu_custom_call" | custom-call | tf_op jit(solution)/shard_map/langevin/pallas_call | solution.py:200
  364.0 0.9 copy_bitcast_fusion
  (4 shorter events, 0.1 us)
Async XLA Ops:
  221.2 5.7 %copy-start.3 = (f32[64]{0:T(128)S(1)}, f32[64]{0:T(128)}, u32[]{:S(2)}) copy-start(f32[64]{0:T(128)} %param.11) | copy-start | bytes 772
  223.9 2.8 copy-start
  223.9 2.9 copy-start.1
  223.9 2.9 copy-start.2
where the time goes:
time: 365 us
  blocking collectives  213 us (58%)
  Pallas kernels  137 us (38%)
  local copies, waits for them, and re-layouts  13.6 us (4%)
    all_gather x1, blocking collectives, on_device(): every = lax.all_gather(flat, ('gx', 'gy'), axis=0)  213 us
    pallas_call x1, Pallas kernels, on_device(): pl.pallas_call(kernel, out_shape=(planes, planes), in_specs=[vmem] * 6, o...  137 us

commit v1 on v0

--- a/solution.py
+++ b/solution.py
@@ -98,14 +98,17 @@
             made = jnp.dot(taps, weights[c], preferred_element_type=jnp.float32)
             slim_parts[c] = made.reshape(2, rows, lanes)
 
-    def banded(source, which, target, wide_one):
+    def banded(source, which, target, wide_one, flipped):
         target[...] = jnp.zeros_like(target)
         span = 6 if wide_one else 4
 
         @pl.loop(0, 9)
         def _(tap):
             c, a = tap // 3, lax.rem(tap, 3)
-            taps = [source[which, a, b, c] for b in range(3)]
+            taps = [
+                source[which, 2 - a, 2 - b, 2 - c] if flipped else source[which, a, b, c]
+                for b in range(3)
+            ]
             zero = jnp.zeros((half, half), jnp.bfloat16)
             pairs = [
                 jnp.concatenate([taps[b] if b < 3 else zero, taps[b - 1] if b > 0 else zero], axis=1)
@@ -116,10 +119,10 @@
                     start = pl.multiple_of(a * (span * half) + (2 * group + b) * half, half)
                     target[c, pl.ds(start, half), group * lanes : (group + 1) * lanes] = pairs[b]
 
-    banded(filters, 0, wide_in, True)
-    banded(filters, 1, slim_out, False)
-    banded(adjoints, 1, wide_out, True)
-    banded(adjoints, 0, slim_in, False)
+    banded(filters, 0, wide_in, True, False)
+    banded(filters, 1, slim_out, False, False)
+    banded(adjoints, 1, wide_out, True, True)
+    banded(adjoints, 0, slim_in, False, True)
 
     for x in range(2):
         q[x] = position[x].T
@@ -168,6 +171,75 @@
         out_momentum[x] = p[x].T
 
 
+def gather_kernel(piece, every, line_send, line_recv, send_sem, recv_sem, own_sem):
+    gx, gy = lax.axis_index("gx"), lax.axis_index("gy")
+    nx, ny = lax.axis_size("gx"), lax.axis_size("gy")
+    right, left = lax.rem(gx + 1, nx), lax.rem(gx + nx - 1, nx)
+    barrier = pltpu.get_barrier_semaphore()
+    for j in range(1, ny):
+        pl.semaphore_signal(barrier, inc=1, device_id={"gy": lax.rem(gy + j, ny)}, device_id_type=MESH)
+    for x in (left, right):
+        pl.semaphore_signal(barrier, inc=1, device_id={"gx": x}, device_id_type=MESH)
+    pl.semaphore_wait(barrier, ny + 1)
+
+    line = [
+        pltpu.make_async_remote_copy(
+            src_ref=piece, dst_ref=every.at[gx, gy],
+            send_sem=line_send.at[j], recv_sem=line_recv.at[j],
+            device_id={"gy": lax.rem(gy + j, ny)}, device_id_type=MESH,
+        )
+        for j in range(1, ny)
+    ]
+    line.append(pltpu.make_async_copy(piece, every.at[gx, gy], own_sem))
+    for copy in line:
+        copy.start()
+    for copy in line:
+        copy.wait()
+
+    def passed(way, step):
+        owner = lax.rem(gx - step + nx, nx) if way == 0 else lax.rem(gx + step, nx)
+        return pltpu.make_async_remote_copy(
+            src_ref=every.at[owner], dst_ref=every.at[owner],
+            send_sem=send_sem.at[way, step], recv_sem=recv_sem.at[way, step],
+            device_id={"gx": right if way == 0 else left}, device_id_type=MESH,
+        )
+
+    both = (nx - 1) // 2
+
+    @pl.loop(0, both)
+    def _(step):
+        copies = [passed(way, step) for way in range(2)]
+        for copy in copies:
+            copy.start()
+        for copy in copies:
+            copy.wait()
+
+    if nx % 2 == 0:
+        copy = passed(0, both)
+        copy.start()
+        copy.wait()
+
+
+def gathered(piece):
+    nx, ny = lax.axis_size("gx"), lax.axis_size("gy")
+    vmem = pl.BlockSpec(memory_space=pltpu.VMEM)
+    return pl.pallas_call(
+        gather_kernel,
+        out_shape=jax.ShapeDtypeStruct((nx, ny, *piece.shape), piece.dtype),
+        in_specs=[vmem],
+        out_specs=vmem,
+        scratch_shapes=[
+            pltpu.SemaphoreType.DMA((ny,)),
+            pltpu.SemaphoreType.DMA((ny,)),
+            pltpu.SemaphoreType.DMA((2, nx // 2)),
+            pltpu.SemaphoreType.DMA((2, nx // 2)),
+            pltpu.SemaphoreType.DMA,
+        ],
+        compiler_params=pltpu.CompilerParams(collective_id=1, has_side_effects=True),
+        name="gather",
+    )(piece)
+
+
 def on_device(position, momentum, noise, filter_in, filter_out, bias):
     channels, nx, ny, depth = position.shape
     steps = noise.shape[0]
@@ -176,13 +248,13 @@
 
     own = jnp.stack([filter_in, filter_out])
     two, o_own, i_own = own.shape[:3]
-    flat = own.reshape(two, o_own, i_own, 27)
-    every = lax.all_gather(flat, ("gx", "gy"), axis=0)
+    taps_first = jnp.transpose(own.reshape(two, o_own, i_own, 27), (3, 0, 1, 2)).reshape(27, -1)
+    spare = -27 % (16 * 128 // taps_first.shape[1])
+    piece = jnp.pad(taps_first, ((0, spare), (0, 0))).reshape(-1, 128)
     parts_x, parts_y = lax.axis_size("gx"), lax.axis_size("gy")
-    every = every.reshape(parts_x, parts_y, two, o_own, i_own, 27)
-    natural = jnp.transpose(every, (2, 5, 0, 3, 1, 4)).reshape(two, 3, 3, 3, channels, channels)
-    adjoints = jnp.flip(natural, (1, 2, 3))
-    filters = jnp.swapaxes(natural, -1, -2)
+    every = gathered(piece).reshape(parts_x, parts_y, 27 + spare, two, o_own, i_own)[:, :, :27]
+    adjoints = jnp.transpose(every, (3, 2, 0, 4, 1, 5)).reshape(two, 3, 3, 3, channels, channels)
+    filters = jnp.swapaxes(adjoints, -1, -2)
 
     def to_planes(block):
         return jnp.transpose(block, (1, 2, 0, 3)).reshape(nx, lanes, depth)

time: 365 us -> 210 us (0.58)
  blocking collectives: 213 us -> 0 us
  Pallas kernels: 137 us -> 191 us
  local copies, waits for them, and re-layouts: 13.6 us -> 18.5 us
    all_gather x1 -> x0, blocking collectives: 213 us -> none  [on_device(): every = lax.all_gather(flat, ('gx', 'gy'), axis=0)]
    pallas_call x0 -> x1, Pallas kernels: none -> 91.3 us  [gathered(): pl.pallas_call(gather_kernel, out_shape=jax.ShapeDtypeStruct((nx, ny, *pi...]
    pallas_call x1, Pallas kernels: 137 us -> 99.3 us  [on_device(): pl.pallas_call(kernel, out_shape=(planes, planes), in_specs=[vmem] * 6, o...]
    transpose x1 -> x2, local copies, waits for them, and re-layouts: 6.94 us -> 7.46 us  [on_device(): jnp.transpose(every, (3, 2, 0, 4, 1, 5))]
where the time goes in v1:
time: 210 us
  Pallas kernels  191 us (91%)
  local copies, waits for them, and re-layouts  18.5 us (9%)
    pallas_call x1, Pallas kernels, on_device(): pl.pallas_call(kernel, out_shape=(planes, planes), in_specs=[vmem] * 6, o...  99.3 us
    pallas_call x1, Pallas kernels, gathered(): pl.pallas_call(gather_kernel, out_shape=jax.ShapeDtypeStruct((nx, ny, *pi...  91.3 us
    transpose x2, local copies, waits for them, and re-layouts, on_device(): jnp.transpose(every, (3, 2, 0, 4, 1, 5))  7.46 us
    reshape x2, local copies, waits for them, and re-layouts, on_device(): jnp.transpose(every, (3, 2, 0, 4, 1, 5))  5.22 us

profile of v1, /device:TPU:33, one launch (start us, length us, event | category | flops | bytes accessed | tf_op | source)
XLA Modules:
  0.0 209.8 jit_solution(1012871930692552867)
XLA Ops:
  0.6 0.8 copy.19
  1.4 0.8 copy.20
  2.2 0.1 copy.27
  2.4 0.7 reshape.41.piece
  3.0 91.3 %gather.1 = bf16[32,4,16,128]{3,2,1,0:T(8,128)(2,1)} custom-call(bf16[16,128]{1,0:T(8,128)(2,1)} %reshape.41.piece), custom_call_target="tpu_custom_call" | custom-call | tf_op jit(solution)/shard_map/gather/pallas_call | solution.py:226
  94.4 2.0 copy.22
  96.4 1.7 slice_bitcast_fusion
  98.1 5.8 %copy.23 = bf16[2,27,32,2,4,16]{5,4,3,2,1,0:T(4,128)(2,1)} copy(bf16[2,27,32,2,4,16]{2,5,3,0,1,4:T(8,128)(2,1)} %slice_bitcast_fusion) | data formatting | bytes 884736 | tf_op jit(solution)/shard_map/transpose | solution.py:256
  103.9 0.0 copy-start
  103.9 4.6 %reshape.43.adjoints = bf16[2,3,3,3,64,64]{5,4,3,2,1,0:T(8,128)(2,1)S(1)} reshape(bf16[2,27,32,2,4,16]{5,4,3,2,1,0:T(4,128)(2,1)} %copy.23) | data formatting | bytes 884736 | tf_op jit(solution)/shard_map/reshape | solution.py:256
  108.5 0.0 copy-start.1
  108.5 0.0 copy-start.2
  108.5 0.0 copy-start.3
  108.6 0.6 copy.24
  109.2 0.0 copy-done
  109.2 0.2 copy-done.1
  109.4 0.1 copy-done.2
  109.5 0.0 copy-done.3
  109.5 0.1 reshape_tile.3.bias
  109.6 99.3 %langevin.1 = (f32[2,128,128]{2,1,0:T(8,128)S(1)}, f32[2,128,128]{2,1,0:T(8,128)S(1)}) custom-call(f32[2,128,128]{2,1,0:T(8,128)S(1)} %bitcast.23, f32[2,128,128]{2,1,0:T(8,128)S(1)} %bitcast.24, bf16[3,2,128,128]{3,2,1,0:T(8,128)(2,1)S(1)} %bitcast.22, bf16[2,3,3,3,64,64]{5,4,3,2,1,0:T(8,128)(2,1)S(1)} %bitcast.21, ...), custom_call_target="tpu_custom_call" | custom-call | tf_op jit(solution)/shard_map/langevin/pallas_call | solution.py:272
  208.9 0.9 copy_bitcast_fusion
  (6 shorter events, 0.1 us)
Async XLA Ops:
  103.9 5.3 %copy-start = (bf16[3,64,2,2,128]{4,3,2,1,0:T(2,128)(2,1)S(1)}, bf16[3,64,2,2,128]{4,3,2,1,0:T(2,128)(2,1)}, u32[]{:S(2)}) copy-start(bf16[3,64,2,2,128]{4,3,2,1,0:T(2,128)(2,1)} %param.8) | copy-start | bytes 589828
  108.5 0.9 copy-start.1
  108.5 1.0 copy-start.2
  108.5 1.0 copy-start.3
